TPU v7x, 32 devices: a whole 2x2x4 slice. The times are simulated.
32 devices in a mesh: dp: 8 (over y, x, core), tp: 4 (over z).
Axes of the slice: x: 2, y: 2, z: 4, core: 2. Of those that a mesh axis runs over, the one named last changes fastest.
Arguments:
- tokens: bfloat16 [4096, 4096], P(('dp', 'tp')), may hold values from -6 to 6
- norm_gain: float32 [4096], replicated, may hold values from 0.1 to 1.9
- w_query: bfloat16 [4096, 4096], P(None, 'tp'), may hold values from -0.09375 to 0.09375
- w_key: bfloat16 [4096, 1024], P(None, 'tp'), may hold values from -2.34375 to 2.34375
- w_value: bfloat16 [4096, 1024], P(None, 'tp'), may hold values from -0.09375 to 0.09375
- w_output: bfloat16 [4096, 4096], P('tp'), may hold values from -0.09375 to 0.09375
- doc_lengths: int32 [32], replicated, may hold values from 1 to 512, as said below
- pack_index: int32 [4096], replicated, may hold values from 0 to 4095, as said below
Outputs:
- output: bfloat16 [4096, 4096], P(('dp', 'tp'))
Inputs may be any that keep to these rules, and one draw needn't show every extreme that they name: `doc_lengths`: each run of 4 documents numbered g * 4 to g * 4 + 4 - 1 (the documents of group g) holds at most 1024 tokens together, and some group holds exactly 1024. No document is longer than 512 tokens, and one has exactly that many. `pack_index`: each packed position appears once. The 128 rows of one device hold at most 32 tokens of the documents of any one group; every device holds the same number of one group's tokens, up to one.
All inputs are finite; a program needn't handle non-finite values.
Results may differ from a plain program's by a relative error of at most 0.01.
Values may be sent and summed in bfloat16 or wider, within the bound.
A program may use at most 128 MiB of HBM per device.

v0:
```python
import jax
import jax.numpy as jnp
from jax import lax
from jax.sharding import PartitionSpec as P

HEAD_DIM = 128
GROUP_DOCS = 4


rope_base = 500000.0
norm_eps = 1e-05
score_floor = -1e30


def row_tables(pack_index, doc_lengths, group_count, tok_dev):
    doc_ends = jnp.cumsum(doc_lengths)
    doc_starts = doc_ends - doc_lengths
    inside = (
        (pack_index[:, None] >= doc_starts[None, :]) & (pack_index[:, None] < doc_ends[None, :])
    ).astype(jnp.int32)
    doc_index = jnp.sum(inside * jnp.arange(doc_lengths.shape[0], dtype=jnp.int32)[None, :], axis=1)
    position = pack_index - jnp.sum(inside * doc_starts[None, :], axis=1)
    owner_group = doc_index // GROUP_DOCS
    member = (
        owner_group.reshape(-1, tok_dev)[:, :, None]
        == jnp.arange(group_count, dtype=jnp.int32)[None, None, :]
    ).astype(jnp.int32)
    slot_rank = jnp.sum((jnp.cumsum(member, axis=1) - 1) * member, axis=2)
    return (doc_index, position, owner_group, slot_rank.reshape(-1))


def rotate(projected, position, head_count):
    row_count = projected.shape[0]
    half_dim = HEAD_DIM // 2
    spread = projected.reshape(row_count, head_count, HEAD_DIM)
    frequency = rope_base ** (-2.0 * jnp.arange(half_dim, dtype=jnp.float32) / HEAD_DIM)
    angles = position.astype(jnp.float32)[:, None] * frequency[None, :]
    cosine = jnp.cos(angles)[:, None, :]
    sine = jnp.sin(angles)[:, None, :]
    lower_part = spread[:, :, :half_dim]
    upper_part = spread[:, :, half_dim:]
    turned = jnp.concatenate(
        [lower_part * cosine - upper_part * sine, upper_part * cosine + lower_part * sine], axis=2
    )
    return turned.reshape(row_count, head_count * HEAD_DIM)


def attend(query, key_rows, value_rows, segment, places, head_count, kv_count):
    slot_total = query.shape[0]
    group_size = head_count // kv_count
    score_scale = HEAD_DIM ** (-0.5)
    block_rows = min(512, slot_total)
    query_heads = query.reshape(slot_total, kv_count, group_size, HEAD_DIM)
    key_heads = key_rows.reshape(slot_total, kv_count, HEAD_DIM)
    value_heads = value_rows.reshape(slot_total, kv_count, HEAD_DIM)
    outputs = []
    for block_start in range(0, slot_total, block_rows):
        query_block = query_heads[block_start : block_start + block_rows]
        score_values = (
            jnp.einsum("qkgd,skd->kgqs", query_block, key_heads, preferred_element_type=jnp.float32)
            * score_scale
        )
        block_segment = segment[block_start : block_start + block_rows]
        block_places = places[block_start : block_start + block_rows]
        allowed = (block_segment[:, None] == segment[None, :]) & (
            places[None, :] <= block_places[:, None]
        )
        score_values = jnp.where(allowed[None, None], score_values, score_floor)
        row_peak = jnp.max(score_values, axis=-1, keepdims=True)
        weights = jnp.exp(score_values - row_peak)
        weights = (weights / jnp.sum(weights, axis=-1, keepdims=True)).astype(jnp.bfloat16)
        mixed_values = jnp.einsum(
            "kgqs,skd->qkgd", weights, value_heads, preferred_element_type=jnp.float32
        )
        outputs.append(mixed_values.astype(jnp.bfloat16).reshape(block_rows, head_count * HEAD_DIM))
    return jnp.concatenate(outputs, axis=0)


def body(tokens, norm_gain, w_query, w_key, w_value, w_output, doc_lengths, pack_index):
    group_count = lax.axis_size("dp")
    tp_count = lax.axis_size("tp")
    tok_dev = tokens.shape[0]
    model_width = tokens.shape[1]
    send_slots = 2 * tok_dev // group_count
    device_total = group_count * tp_count
    slot_total = device_total * send_slots
    group_rows = group_count * send_slots
    my_group = lax.axis_index("dp")
    my_source = my_group * tp_count + lax.axis_index("tp")
    doc_index, position, owner_group, slot_rank = row_tables(
        pack_index, doc_lengths, group_count, tok_dev
    )
    own_group = lax.dynamic_slice_in_dim(owner_group, my_source * tok_dev, tok_dev)
    own_rank = lax.dynamic_slice_in_dim(slot_rank, my_source * tok_dev, tok_dev)
    send_index = own_group * send_slots + own_rank
    residual = tokens.astype(jnp.float32)
    normed = (
        residual
        * lax.rsqrt(jnp.mean(residual * residual, axis=1, keepdims=True) + norm_eps)
        * norm_gain
    ).astype(jnp.bfloat16)
    outgoing = jnp.zeros((group_rows, model_width), jnp.bfloat16).at[send_index].set(normed)
    fanned = jnp.broadcast_to(
        outgoing.reshape(group_count, 1, send_slots, model_width),
        (group_count, tp_count, send_slots, model_width),
    )
    arrived = lax.all_to_all(
        fanned.reshape(slot_total, model_width),
        ("dp", "tp"),
        split_axis=0,
        concat_axis=0,
        tiled=True,
    )
    mine = (owner_group == my_group).reshape(device_total, tok_dev)
    slot_match = (
        slot_rank.reshape(device_total, tok_dev)[:, :, None]
        == jnp.arange(send_slots, dtype=jnp.int32)[None, None, :]
    )
    pick = (mine[:, :, None] & slot_match).astype(jnp.int32)
    occupied = jnp.sum(pick, axis=1).reshape(slot_total)
    slot_doc = jnp.sum(pick * doc_index.reshape(device_total, tok_dev, 1), axis=1).reshape(
        slot_total
    )
    slot_place = jnp.sum(pick * position.reshape(device_total, tok_dev, 1), axis=1).reshape(
        slot_total
    )
    segment = jnp.where(occupied > 0, slot_doc, -1 - jnp.arange(slot_total, dtype=jnp.int32))
    head_count = w_query.shape[1] // HEAD_DIM
    kv_count = w_key.shape[1] // HEAD_DIM
    query = rotate(
        jnp.dot(arrived, w_query, preferred_element_type=jnp.float32), slot_place, head_count
    ).astype(jnp.bfloat16)
    key_rows = rotate(
        jnp.dot(arrived, w_key, preferred_element_type=jnp.float32), slot_place, kv_count
    ).astype(jnp.bfloat16)
    value_rows = jnp.dot(arrived, w_value, preferred_element_type=jnp.float32).astype(jnp.bfloat16)
    context = attend(query, key_rows, value_rows, segment, slot_place, head_count, kv_count)
    came_back = lax.all_to_all(context, "dp", split_axis=0, concat_axis=0, tiled=True)
    group_span = tp_count * tok_dev
    group_owner = lax.dynamic_slice_in_dim(owner_group, my_group * group_span, group_span)
    group_rank = lax.dynamic_slice_in_dim(slot_rank, my_group * group_span, group_span)
    source_member = jnp.arange(group_span, dtype=jnp.int32) // tok_dev
    fetch_index = group_owner * (tp_count * send_slots) + source_member * send_slots + group_rank
    compact = jnp.take(came_back, fetch_index, axis=0)
    attended = lax.psum_scatter(
        jnp.dot(compact, w_output, preferred_element_type=jnp.float32).astype(jnp.bfloat16),
        "tp",
        scatter_dimension=0,
        tiled=True,
    ).astype(jnp.float32)
    return (residual + attended).astype(jnp.bfloat16)


def solution(mesh):
    placed = (
        P(("dp", "tp"), None),
        P(),
        P(None, "tp"),
        P(None, "tp"),
        P(None, "tp"),
        P("tp", None),
        P(),
        P(),
    )
    return jax.shard_map(
        body, mesh=mesh, in_specs=placed, out_specs=P(("dp", "tp"), None), check_vma=False
    )
```

profile of v0, /device:TPU:0, one launch (start us, length us, event | category | flops | bytes accessed | tf_op | source)
XLA Modules:
  0.0 409.7 jit_solution(11714394760156499715)
XLA Ops:
  9.4 3.3 select_reduce_fusion
  14.4 4.0 scatter_custom_fusion
  18.4 5.9 %broadcast_in_dim.39 = bf16[8,4,32,4096]{3,2,1,0:T(8,128)(2,1)} broadcast(bf16[8,32,4096]{2,1,0:T(8,128)(2,1)} %bitcast.90), dimensions={0,2,3} | broadcast | bytes 10485760 | tf_op jit(solution)/shard_map/broadcast_in_dim | solution.py:103
  24.2 7.6 %all-to-all-start = ((bf16[32,32,4096]{2,1,0:T(8,128)(2,1)}), bf16[32,32,4096]{2,1,0:T(8,128)(2,1)}, u32[]{:S(2)}, u32[]{:S(2)}) async-start(bf16[32,32,4096]{2,1,0:T(8,128)(2,1)} %bitcast.89), calls=%async_computation | async-start | bytes 16777216 | tf_op jit(solution)/shard_map/all_to_all | solution.py:107
  31.9 1.7 select_reduce_fusion.3
  34.0 11.3 %copy.80 = bf16[1024,4096]{1,0:T(8,128)(2,1)} copy(bf16[1024,4096]{0,1:T(8,128)(2,1)} %bitcast.91) | data formatting | bytes 16777216 | tf_op jit(solution)/shard_map/dot_general | solution.py:131
  45.3 4.1 %copy.77 = bf16[256,4096]{1,0:T(8,128)(2,1)} copy(bf16[256,4096]{0,1:T(8,128)(2,1)} %bitcast.94) | data formatting | bytes 4194304 | tf_op jit(solution)/shard_map/dot_general | solution.py:134
  49.4 1.8 multiply_cosine_fusion
  51.2 2.0 compare_and_fusion.1
  53.1 159.9 %all-to-all-done = bf16[32,32,4096]{2,1,0:T(8,128)(2,1)} async-done(((bf16[32,32,4096]{2,1,0:T(8,128)(2,1)}), bf16[32,32,4096]{2,1,0:T(8,128)(2,1)}, u32[]{:S(2)}, u32[]{:S(2)}) %all-to-all-start) | async-done | bytes 8388640 | tf_op jit(solution)/shard_map/all_to_all | solution.py:107
  213.1 13.0 %fusion.55 = f32[1024,8,128]{0,2,1:T(8,128)S(1)} fusion(bf16[1024,4096,1]{1,0,2:T(8,128)(2,1)} %bitcast.10, bf16[8,128,4096]{2,1,0:T(8,128)(2,1)} %bitcast.92), kind=kOutput, calls=%fused_computation.111 | convolution fusion | flops 8589934592 | bytes 20971520 | tf_op jit(solution)/shard_map/dot_general | solution.py:131
  226.1 5.8 %fusion.54 = f32[1024,2,128]{0,2,1:T(8,128)S(1)} fusion(bf16[1024,4096,1]{1,0,2:T(8,128)(2,1)} %bitcast.10, bf16[2,128,4096]{2,1,0:T(8,128)(2,1)S(1)} %bitcast.95), kind=kOutput, calls=%fused_computation.110 | convolution fusion | flops 2147483648 | bytes 11534336 | tf_op jit(solution)/shard_map/dot_general | solution.py:134
  233.7 6.5 %convolution_convert_fusion.1 = bf16[1024,256]{0,1:T(8,128)(2,1)} fusion(bf16[1024,4096]{1,0:T(8,128)(2,1)} %bitcast.5, bf16[4096,256]{1,0:T(8,128)(2,1)S(1)} %copy-done), kind=kOutput, calls=%fused_computation.43 | convolution fusion | flops 2147745792 | bytes 11010048 | tf_op jit(solution)/shard_map/dot_general | solution.py:136
  241.2 10.9 %fusion.52 = (f32[2,4,512]{2,1,0:T(4,128)S(1)}, f32[2,4,512,1024]{2,3,1,0:T(8,128)}) fusion(pred[512,1024]{0,1:T(8,128)(4,1)} %get-tuple-element.21, bf16[512,2,4,128]{0,3,2,1:T(8,128)(2,1)S(1)} %bitcast.97, bf16[1024,2,64]{0,2,1:T(8,128)(2,1)} %get-tuple-element.17, bf16[1024,2,64]{0,2,1:T(8,128)(2,1)S(1)} %copy-done.5), kind=kOutput, calls=%fused_computation.108 | convolution fusion | flops 1091568640 | bytes 18890752 | tf_op jit(solution)/shard_map/sub | solution.py:70
  252.1 11.2 %fusion.53 = (f32[2,4,512]{2,1,0:T(4,128)S(1)}, f32[2,4,512,1024]{2,3,1,0:T(8,128)}) fusion(pred[512,1024]{0,1:T(8,128)(4,1)} %get-tuple-element.20, bf16[512,2,4,128]{0,3,2,1:T(8,128)(2,1)S(1)} %bitcast.96, bf16[1024,2,64]{0,2,1:T(8,128)(2,1)} %get-tuple-element.17, bf16[1024,2,64]{0,2,1:T(8,128)(2,1)S(1)} %copy-done.5), kind=kOutput, calls=%fused_computation.109 | convolution fusion | flops 1091568640 | bytes 18890752 | tf_op jit(solution)/shard_map/sub | solution.py:70
  263.3 7.2 %fusion.22 = bf16[2,128,4,512]{3,1,2,0:T(8,128)(2,1)S(1)} fusion(bf16[1024,2,128,1]{0,2,3,1:T(8,128)(2,1)S(1)} %bitcast.104, f32[2,4,512,1024]{2,3,1,0:T(8,128)} %get-tuple-element.27, f32[2,4,512]{2,1,0:T(4,128)S(1)} %get-tuple-element.26), kind=kOutput, calls=%fused_computation.41 | convolution fusion | flops 1082654720 | bytes 18366464 | tf_op jit(solution)/shard_map/kgqs,skd->qkgd/dot_general | solution.py:72
  270.5 3.3 copy-done.8
  275.6 2.6 copy.83
  278.2 4.2 %all-to-all-start.1 = ((bf16[8,128,1024]{2,1,0:T(8,128)(2,1)}), bf16[8,128,1024]{2,1,0:T(8,128)(2,1)S(1)}, u32[]{:S(2)}, u32[]{:S(2)}) async-start(bf16[8,128,1024]{2,1,0:T(8,128)(2,1)} %bitcast.93), calls=%async_computation.1 | async-start | bytes 4194304 | tf_op jit(solution)/shard_map/all_to_all | solution.py:138
  282.6 26.5 %all-to-all-done.1 = bf16[8,128,1024]{2,1,0:T(8,128)(2,1)S(1)} async-done(((bf16[8,128,1024]{2,1,0:T(8,128)(2,1)}), bf16[8,128,1024]{2,1,0:T(8,128)(2,1)S(1)}, u32[]{:S(2)}, u32[]{:S(2)}) %all-to-all-start.1) | async-done | bytes 2097184 | tf_op jit(solution)/shard_map/all_to_all | solution.py:138
  309.1 2.8 gather_fusion
  311.8 10.2 %convolution_convert_fusion = bf16[512,4096]{1,0:T(8,128)(2,1)} fusion(bf16[1024,4096]{1,0:T(8,128)(2,1)} %param.13, bf16[512,1024]{1,0:T(8,128)(2,1)} %gather_fusion, pred[512]{0:T(512)(128)(4,1)S(1)} %get-tuple-element.10), kind=kOutput, calls=%fused_computation.20 | convolution fusion | flops 4297588736 | bytes 13632000 | tf_op jit(solution)/shard_map/dot_general | solution.py:146
  322.1 78.4 %reduce-scatter.2.cloned.1.call-done = bf16[128,4096]{1,0:T(8,128)(2,1)} async-done(((bf16[512,4096]{1,0:T(8,128)(2,1)}), bf16[128,4096]{1,0:T(8,128)(2,1)}) %reduce-scatter.2.cloned.1.call-update) | async-done | bytes 1048592 | tf_op jit(solution)/shard_map/reduce_scatter | solution.py:145
  400.4 2.4 fusion.15
  (51 shorter events, 9.6 us)
Async XLA Ops:
  6.5 227.1 %copy-start = (bf16[4096,256]{1,0:T(8,128)(2,1)S(1)}, bf16[4096,256]{1,0:T(8,128)(2,1)}, u32[]{:S(2)}) copy-start(bf16[4096,256]{1,0:T(8,128)(2,1)} %param.12) | copy-start | bytes 6291460
  6.5 7.8 %copy-start.2 = (bf16[128,4096]{1,0:T(8,128)(2,1)S(1)}, bf16[128,4096]{1,0:T(8,128)(2,1)}, u32[]{:S(2)}) copy-start(bf16[128,4096]{1,0:T(8,128)(2,1)} %param.8) | copy-start | bytes 3145732
  24.2 7.7 %copy-start.6 = (s32[4096]{0:T(1024)S(1)}, s32[4096]{0:T(1024)}, u32[]{:S(2)}) copy-start(s32[4096]{0:T(1024)} %param.15) | copy-start | bytes 49156
  24.2 188.8 %all-to-all-start = ((bf16[32,32,4096]{2,1,0:T(8,128)(2,1)}), bf16[32,32,4096]{2,1,0:T(8,128)(2,1)}, u32[]{:S(2)}, u32[]{:S(2)}) async-start(bf16[32,32,4096]{2,1,0:T(8,128)(2,1)} %bitcast.89), calls=%async_computation | async-start | bytes 16777216 | tf_op jit(solution)/shard_map/all_to_all | solution.py:107
  213.1 13.0 %copy-start.4 = (bf16[256,4096]{1,0:T(8,128)(2,1)S(1)}, bf16[256,4096]{1,0:T(8,128)(2,1)}, u32[]{:S(2)}) copy-start(bf16[256,4096]{1,0:T(8,128)(2,1)} %copy.77) | copy-start | bytes 6291460
  226.1 5.8 %copy-start.3 = (f32[1024,64]{0,1:T(8,128)S(1)}, f32[1024,64]{0,1:T(8,128)}, u32[]{:S(2)}) copy-start(f32[1024,64]{0,1:T(8,128)} %get-tuple-element.23) | copy-start | bytes 786436
  240.2 0.9 copy-start.5
  252.1 11.2 %copy-start.7 = (bf16[1024,256]{0,1:T(8,128)(2,1)S(1)}, bf16[1024,256]{0,1:T(8,128)(2,1)}, u32[]{:S(2)}) copy-start(bf16[1024,256]{0,1:T(8,128)(2,1)} %convolution_convert_fusion.1) | copy-start | bytes 1572868
  263.3 10.5 %copy-start.8 = (f32[2,4,512,1024]{2,3,1,0:T(8,128)S(1)}, f32[2,4,512,1024]{2,3,1,0:T(8,128)}, u32[]{:S(2)}) copy-start(f32[2,4,512,1024]{2,3,1,0:T(8,128)} %get-tuple-element.29) | copy-start | bytes 50331652
  278.2 30.8 %all-to-all-start.1 = ((bf16[8,128,1024]{2,1,0:T(8,128)(2,1)}), bf16[8,128,1024]{2,1,0:T(8,128)(2,1)S(1)}, u32[]{:S(2)}, u32[]{:S(2)}) async-start(bf16[8,128,1024]{2,1,0:T(8,128)(2,1)} %bitcast.93), calls=%async_computation.1 | async-start | bytes 4194304 | tf_op jit(solution)/shard_map/all_to_all | solution.py:138
  282.4 118.0 %reduce-scatter.2.cloned.1.call-start = ((), (), s32[]{:S(2)}) async-start(), calls=%async_computation.3 | async-start | bytes 5242880 | tf_op jit(solution)/shard_map/reduce_scatter | solution.py:145
  322.0 80.8 %copy-start.1 = (bf16[4096,256]{1,0:T(8,128)(2,1)S(1)}, bf16[4096,256]{1,0:T(8,128)(2,1)}, u32[]{:S(2)}) copy-start(bf16[4096,256]{1,0:T(8,128)(2,1)} %param.12) | copy-start | bytes 6291460
Sparse Core Ops, SparseCore 0:
  322.2 78.2 reduce-scatter.1
where the time goes:
time: 411 us; the launch traced here: 410 us
  waiting for transfers between devices  265 us (64%)
  matrix products  66.4 us (16%)
  local copies, waits for them, and re-layouts  32.1 us (8%)
  other arithmetic  21 us (5%)
  between operations  13.6 us (3%)
  starting transfers between devices  11.9 us (3%)
    all_to_all x1, waiting for transfers between devices, body(): lax.all_to_all(fanned.reshape(slot_total, model_width), ('dp', 'tp'), spl...  160 us
    reduce_scatter x1, waiting for transfers between devices, body(): lax.psum_scatter(jnp.dot(compact, w_output, preferred_element_type=jnp.fl...  78.4 us
    all_to_all x1, waiting for transfers between devices, body(): lax.all_to_all(context, 'dp', split_axis=0, concat_axis=0, tiled=True)  26.5 us
    sub x2, matrix products, attend(): weights = jnp.exp(score_values - row_peak)  22.1 us
    dot_general x1, matrix products, body(): jnp.dot(arrived, w_query, preferred_element_type=jnp.float32)  13 us
    dot_general x1, local copies, waits for them, and re-layouts, body(): jnp.dot(arrived, w_query, preferred_element_type=jnp.float32)  11.3 us
    dot_general x1, matrix products, body(): jnp.dot(compact, w_output, preferred_element_type=jnp.float32)  10.2 us
    dot_general x2, matrix products, attend(): jnp.einsum('kgqs,skd->qkgd', weights, value_heads, preferred_element_type...  8.7 us
  transfers between devices with their start and end apart: 3, of which 3 were waited for; matrix products, arithmetic and copies ran while one was open for 5% of the time, Pallas kernels for 0%

commit v1 on v0

v1 whole, which is shorter than its diff:
```python
import functools

import jax
import jax.numpy as jnp
from jax import lax
from jax.experimental import pallas as pl
from jax.experimental.pallas import tpu as pltpu
from jax.sharding import PartitionSpec as P

HEAD_DIM = 128
GROUP_DOCS = 4
LOG2E = 1.4426950408889634

rope_base = 500000.0
norm_eps = 1e-05
score_floor = -1e30
VMEM_BYTES = 60 * 1024 * 1024
MESH = pl.DeviceIdType.MESH
VMEM_SPEC = pl.BlockSpec(memory_space=pltpu.VMEM)


def remote(src, dst, send_sem, recv_sem, where):
    return pltpu.make_async_remote_copy(
        src_ref=src,
        dst_ref=dst,
        send_sem=send_sem,
        recv_sem=recv_sem,
        device_id=where,
        device_id_type=MESH,
    )


def greet(peers):
    barrier = pltpu.get_barrier_semaphore()
    for where in peers:
        pl.semaphore_signal(barrier, inc=1, device_id=where, device_id_type=MESH)
    pl.semaphore_wait(barrier, len(peers))


def project_kernel(
    exchange, x_ref, wq_ref, wk_ref, wv_ref, cos_ref, sin_ref, sort_ref,
    q_out, kv_out, gathered, mixed_q, mixed_kv, send_sem, recv_sem, kv_send, kv_recv,
):
    tok = x_ref.shape[0]
    half = tok // 2
    dp = lax.axis_index("dp")
    me = lax.axis_index("tp")
    right, left = lax.rem(me + 1, 4), lax.rem(me + 3, 4)
    far = lax.rem(me + 2, 4)
    go_right, go_left = (dp, right), (dp, left)
    core = lax.rem(dp, 2)
    x_at = lax.rem(dp // 2, 2)
    y_at = dp // 4
    mate = dp + 1 - 2 * core
    x_near = dp + 2 - 4 * x_at
    y_near = dp + 4 - 8 * y_at
    peers = [go_right, go_left]
    if exchange:
        peers += [(mate, me), (x_near, me), (y_near, me)]
    greet(peers)

    def rows(owner, start=0, size=tok):
        return pl.ds(pl.multiple_of(owner * tok + start, size), size)

    own_right = remote(x_ref, gathered.at[rows(me)], send_sem.at[0], recv_sem.at[0], go_right)
    own_left = remote(x_ref, gathered.at[rows(me)], send_sem.at[1], recv_sem.at[1], go_left)
    own_right.start()
    own_left.start()

    def project(owner, block):
        cosine = cos_ref[rows(owner), :]
        sine = sin_ref[rows(owner), :]

        def turn(tile):
            heads = []
            for h in range(tile.shape[1] // HEAD_DIM):
                head = tile[:, h * HEAD_DIM : (h + 1) * HEAD_DIM]
                heads.append(head * cosine + pltpu.roll(head, HEAD_DIM // 2, 1) * sine)
            return jnp.concatenate(heads, axis=1).astype(jnp.bfloat16)

        kv_width = wk_ref.shape[1]
        keys = jnp.dot(block[...], wk_ref[...], preferred_element_type=jnp.float32)
        mixed_kv[rows(owner), pl.ds(0, kv_width)] = turn(keys)
        values = jnp.dot(block[...], wv_ref[...], preferred_element_type=jnp.float32)
        mixed_kv[rows(owner), pl.ds(kv_width, kv_width)] = values.astype(jnp.bfloat16)

        def step(i, _):
            columns = pl.ds(pl.multiple_of(i * 256, 256), 256)
            tile = jnp.dot(block[...], wq_ref[:, columns], preferred_element_type=jnp.float32)
            mixed_q[rows(owner), columns] = turn(tile)
            return 0

        lax.fori_loop(0, wq_ref.shape[1] // 256, step, 0)

    project(me, x_ref)
    own_right.wait_recv()
    top = gathered.at[rows(left, 0, half)]
    pass_right = remote(top, top, send_sem.at[2], recv_sem.at[2], go_right)
    pass_right.start()
    own_left.wait_recv()
    low = gathered.at[rows(right, half, half)]
    pass_left = remote(low, low, send_sem.at[3], recv_sem.at[3], go_left)
    pass_left.start()
    project(left, gathered.at[rows(left)])
    project(right, gathered.at[rows(right)])
    pass_right.wait_recv()
    pass_left.wait_recv()
    project(far, gathered.at[rows(far)])

    own = kv_out.at[dp] if exchange else kv_out.at[0]
    own[...] = jnp.dot(
        sort_ref[...], mixed_kv[...], preferred_element_type=jnp.float32
    ).astype(jnp.bfloat16)
    started = [own_right, own_left, pass_right, pass_left]
    if exchange:
        span = kv_out.shape[1]
        upper, lower = pl.ds(0, span // 2), pl.ds(span // 2, span // 2)
        cross = x_near + y_near - dp

        def put(ref, i, where):
            copy = remote(ref, ref, kv_send.at[i], kv_recv.at[i], (where, me))
            copy.start()
            return copy

        to_x = put(kv_out.at[dp], 0, x_near)
        to_y = put(kv_out.at[dp], 1, y_near)
        to_mate = put(kv_out.at[dp], 2, mate)

    def sort_step(i, _):
        columns = pl.ds(pl.multiple_of(i * 256, 256), 256)
        q_out[:, columns] = jnp.dot(
            sort_ref[...], mixed_q[:, columns], preferred_element_type=jnp.float32
        ).astype(jnp.bfloat16)
        return 0

    lax.fori_loop(0, wq_ref.shape[1] // 256, sort_step, 0)

    if exchange:
        to_x.wait_recv()
        x_over = put(kv_out.at[x_near, upper], 3, y_near)
        x_mate = put(kv_out.at[x_near], 4, mate)
        to_y.wait_recv()
        y_over = put(kv_out.at[y_near, lower], 5, x_near)
        y_mate = put(kv_out.at[y_near], 6, mate)
        x_over.wait_recv()
        up_mate = put(kv_out.at[cross, upper], 7, mate)
        y_over.wait_recv()
        low_mate = put(kv_out.at[cross, lower], 8, mate)
        for copy in (to_mate, x_mate, y_mate, up_mate, low_mate):
            copy.wait_recv()
        started += [to_x, to_y, to_mate, x_over, x_mate, y_over, y_mate, up_mate, low_mate]
    for copy in started:
        copy.wait_send()


def project(normed, w_query, w_key, w_value, cosine, sine, sort, exchange, group_count):
    tok, width = normed.shape
    span = 4 * tok
    q_width, kv_width = w_query.shape[1], w_key.shape[1]
    slots = group_count if exchange else 1
    return pl.pallas_call(
        functools.partial(project_kernel, exchange),
        out_shape=(
            jax.ShapeDtypeStruct((span, q_width), jnp.bfloat16),
            jax.ShapeDtypeStruct((slots, span, 2 * kv_width), jnp.bfloat16),
        ),
        in_specs=[VMEM_SPEC] * 7,
        out_specs=(VMEM_SPEC, VMEM_SPEC),
        scratch_shapes=[
            pltpu.VMEM((span, width), jnp.bfloat16),
            pltpu.VMEM((span, q_width), jnp.bfloat16),
            pltpu.VMEM((span, 2 * kv_width), jnp.bfloat16),
            pltpu.SemaphoreType.DMA((4,)),
            pltpu.SemaphoreType.DMA((4,)),
            pltpu.SemaphoreType.DMA((9,)),
            pltpu.SemaphoreType.DMA((9,)),
        ],
        compiler_params=pltpu.CompilerParams(
            collective_id=0, has_side_effects=True, vmem_limit_bytes=VMEM_BYTES
        ),
        name="project",
    )(normed, w_query, w_key, w_value, cosine, sine, sort)


def attend_kernel(
    key_rows, q_rows, bounds_ref, q_ref, kv_ref, key_place_ref, q_place_ref, q_start_ref, back_ref,
    out_ref, context,
):
    sources = kv_ref.shape[0]
    kv_count = kv_ref.shape[2] // (2 * HEAD_DIM)
    group = q_ref.shape[1] // HEAD_DIM // kv_count
    chunk = sources * key_rows
    scale = HEAD_DIM ** (-0.5) * LOG2E
    stack = group * q_rows

    def tile_step(t, _):
        at = pl.ds(pl.multiple_of(t * q_rows, q_rows), q_rows)
        place = q_place_ref[at, :]
        start = q_start_ref[at, :]
        queries = []
        for h in range(kv_count):
            queries.append(
                jnp.concatenate(
                    [
                        q_ref[at, (h * group + j) * HEAD_DIM : (h * group + j + 1) * HEAD_DIM]
                        for j in range(group)
                    ],
                    axis=0,
                )
            )

        def chunk_step(b, carry):
            places = key_place_ref[b]
            bias = jnp.where(
                (places >= start) & (places <= place), jnp.float32(0), jnp.float32(score_floor)
            )
            bias = jnp.concatenate([bias] * group, axis=0)
            rows = pl.ds(pl.multiple_of(b * key_rows, key_rows), key_rows)
            after = []
            for h in range(kv_count):
                peak, total, mixed = carry[h]
                keys = kv_ref[:, rows, h * HEAD_DIM : (h + 1) * HEAD_DIM].reshape(chunk, HEAD_DIM)
                low = (kv_count + h) * HEAD_DIM
                values = kv_ref[:, rows, low : low + HEAD_DIM].reshape(chunk, HEAD_DIM)
                scores = (
                    lax.dot_general(
                        queries[h], keys, (((1,), (1,)), ((), ())),
                        preferred_element_type=jnp.float32,
                    )
                    * scale
                    + bias
                )
                new_peak = jnp.maximum(peak, jnp.max(scores, axis=1, keepdims=True))
                weights = jnp.exp2(scores - new_peak)
                fade = jnp.exp2(peak - new_peak)
                total = total * fade + jnp.sum(weights, axis=1, keepdims=True)
                mixed = mixed * fade + jnp.dot(
                    weights.astype(jnp.bfloat16), values, preferred_element_type=jnp.float32
                )
                after.append((new_peak, total, mixed))
            return tuple(after)

        first = tuple(
            (
                jnp.full((stack, 1), score_floor, jnp.float32),
                jnp.zeros((stack, 1), jnp.float32),
                jnp.zeros((stack, HEAD_DIM), jnp.float32),
            )
            for _ in range(kv_count)
        )
        last = lax.fori_loop(bounds_ref[0, t], bounds_ref[1, t], chunk_step, first)
        for h in range(kv_count):
            _, total, mixed = last[h]
            done = (mixed / total).astype(jnp.bfloat16)
            for j in range(group):
                head = (h * group + j) * HEAD_DIM
                context[at, head : head + HEAD_DIM] = done[j * q_rows : (j + 1) * q_rows]
        return 0

    lax.fori_loop(0, q_ref.shape[0] // q_rows, tile_step, 0)

    def back_step(i, _):
        columns = pl.ds(pl.multiple_of(i * 256, 256), 256)
        out_ref[:, columns] = jnp.dot(
            back_ref[...], context[:, columns], preferred_element_type=jnp.float32
        ).astype(jnp.bfloat16)
        return 0

    lax.fori_loop(0, q_ref.shape[1] // 256, back_step, 0)


def attend(bounds, query, kv_all, key_place, q_place, q_start, back, key_rows, q_rows):
    return pl.pallas_call(
        functools.partial(attend_kernel, key_rows, q_rows),
        out_shape=jax.ShapeDtypeStruct(query.shape, jnp.bfloat16),
        in_specs=[pl.BlockSpec(memory_space=pltpu.SMEM)] + [VMEM_SPEC] * 6,
        out_specs=VMEM_SPEC,
        scratch_shapes=[pltpu.VMEM(query.shape, jnp.bfloat16)],
        compiler_params=pltpu.CompilerParams(vmem_limit_bytes=VMEM_BYTES),
        name="attend",
    )(bounds, query, kv_all, key_place, q_place, q_start, back)


def output_kernel(
    context_ref, w_ref, tokens_ref, out_ref,
    far_out, right_out, left_out, relay, from_left, from_right, send_sem, recv_sem,
):
    tok, width = tokens_ref.shape
    half = width // 2
    dp = lax.axis_index("dp")
    me = lax.axis_index("tp")
    right, left = lax.rem(me + 1, 4), lax.rem(me + 3, 4)
    far = lax.rem(me + 2, 4)
    go_right, go_left = (dp, right), (dp, left)
    greet([go_right, go_left])
    columns = (pl.ds(0, half), pl.ds(half, half))
    tile = 256

    def fill(owner, dst, side, more=None):
        rows = pl.ds(pl.multiple_of(owner * tok, tok), tok)

        def step(i, _):
            at = pl.ds(pl.multiple_of(side * half + i * tile, tile), tile)
            term = jnp.dot(context_ref[rows, :], w_ref[:, at], preferred_element_type=jnp.float32)
            if more is not None:
                part = pl.ds(pl.multiple_of(i * tile, tile), tile)
                term = term + more[:, part].astype(jnp.float32)
            at_half = pl.ds(pl.multiple_of(i * tile, tile), tile)
            dst[side, :, at_half] = term.astype(jnp.bfloat16)
            return 0

        lax.fori_loop(0, half // tile, step, 0)

    def put(src, dst, i, where):
        copy = remote(src, dst, send_sem.at[i], recv_sem.at[i], where)
        copy.start()
        return copy

    fill(far, far_out, 0)
    far_right = put(far_out.at[0], relay.at[0], 0, go_right)
    fill(far, far_out, 1)
    far_left = put(far_out.at[1], relay.at[1], 1, go_left)
    fill(right, right_out, 1)
    near_right = put(right_out.at[1], from_left.at[1], 2, go_right)
    fill(left, left_out, 0)
    near_left = put(left_out.at[0], from_right.at[0], 3, go_left)
    far_right.wait_recv()
    fill(right, right_out, 0, relay.at[0])
    sum_right = put(right_out.at[0], from_left.at[0], 4, go_right)
    far_left.wait_recv()
    fill(left, left_out, 1, relay.at[1])
    sum_left = put(left_out.at[1], from_right.at[1], 5, go_left)
    near_right.wait_recv()
    near_left.wait_recv()

    rows = pl.ds(pl.multiple_of(me * tok, tok), tok)
    sums = (sum_right, sum_left)
    for copy in sums:
        copy.wait_recv()
    for side in range(2):

        def last_step(i, _):
            at = pl.ds(pl.multiple_of(side * half + i * tile, tile), tile)
            part = pl.ds(pl.multiple_of(i * tile, tile), tile)
            term = jnp.dot(context_ref[rows, :], w_ref[:, at], preferred_element_type=jnp.float32)
            term = term + from_left[side, :, part].astype(jnp.float32)
            term = term + from_right[side, :, part].astype(jnp.float32)
            out_ref[:, at] = (term + tokens_ref[:, at].astype(jnp.float32)).astype(jnp.bfloat16)
            return 0

        lax.fori_loop(0, half // tile, last_step, 0)
    for copy in (far_right, far_left, near_right, near_left, sum_right, sum_left):
        copy.wait_send()


def project_out(context, w_output, tokens):
    tok, width = tokens.shape
    pair = pltpu.VMEM((2, tok, width // 2), jnp.bfloat16)
    return pl.pallas_call(
        output_kernel,
        out_shape=jax.ShapeDtypeStruct(tokens.shape, jnp.bfloat16),
        in_specs=[VMEM_SPEC] * 3,
        out_specs=VMEM_SPEC,
        scratch_shapes=[pair] * 6
        + [pltpu.SemaphoreType.DMA((6,)), pltpu.SemaphoreType.DMA((6,))],
        compiler_params=pltpu.CompilerParams(
            collective_id=1, has_side_effects=True, vmem_limit_bytes=VMEM_BYTES
        ),
        name="project_out",
    )(context, w_output, tokens)


def body(tokens, norm_gain, w_query, w_key, w_value, w_output, doc_lengths, pack_index):
    group_count = lax.axis_size("dp")
    tp_count = lax.axis_size("tp")
    tok_dev = tokens.shape[0]
    span = tp_count * tok_dev
    my_group = lax.axis_index("dp")
    exchange = group_count == 8
    q_rows = 64
    key_rows = max(16, 512 // group_count)
    key_chunks = span // key_rows

    packs = pack_index.reshape(group_count, span)
    order = jnp.arange(span, dtype=jnp.int32)
    rank = jnp.sum((packs[:, None, :] < packs[:, :, None]).astype(jnp.int32), axis=2)
    sorted_packs = jnp.sum(
        jnp.where(rank[:, None, :] == order[None, :, None], packs[:, None, :], 0), axis=2
    )
    key_place = (
        sorted_packs.reshape(group_count, key_chunks, key_rows)
        .transpose(1, 0, 2)
        .reshape(key_chunks, 1, group_count * key_rows)
    )
    chunk_low = jnp.min(key_place, axis=(1, 2))
    chunk_high = jnp.max(key_place, axis=(1, 2))

    doc_ends = jnp.cumsum(doc_lengths)
    doc_starts = doc_ends - doc_lengths

    def start_of(place):
        inside = (place[:, None] >= doc_starts[None, :]) & (place[:, None] < doc_ends[None, :])
        return jnp.sum(jnp.where(inside, doc_starts[None, :], 0), axis=1)

    my_pack = lax.dynamic_index_in_dim(packs, my_group, 0, keepdims=False)
    my_rank = lax.dynamic_index_in_dim(rank, my_group, 0, keepdims=False)
    my_sorted = lax.dynamic_index_in_dim(sorted_packs, my_group, 0, keepdims=False)
    sort = (my_rank[None, :] == order[:, None]).astype(jnp.bfloat16)
    back = (my_rank[:, None] == order[None, :]).astype(jnp.bfloat16)
    my_start = start_of(my_sorted)
    tile_low = my_start.reshape(-1, q_rows)[:, 0]
    tile_high = my_sorted.reshape(-1, q_rows)[:, -1]
    bounds = jnp.stack(
        [
            jnp.sum((chunk_high[None, :] < tile_low[:, None]).astype(jnp.int32), axis=1),
            jnp.sum((chunk_low[None, :] <= tile_high[:, None]).astype(jnp.int32), axis=1),
        ]
    )

    position = my_pack - start_of(my_pack)
    half_dim = HEAD_DIM // 2
    frequency = rope_base ** (-2.0 * jnp.arange(half_dim, dtype=jnp.float32) / HEAD_DIM)
    angles = position.astype(jnp.float32)[:, None] * frequency[None, :]
    cos_half, sin_half = jnp.cos(angles), jnp.sin(angles)
    cosine = jnp.concatenate([cos_half, cos_half], axis=1)
    sine = jnp.concatenate([-sin_half, sin_half], axis=1)

    residual = tokens.astype(jnp.float32)
    normed = (
        residual
        * lax.rsqrt(jnp.mean(residual * residual, axis=1, keepdims=True) + norm_eps)
        * norm_gain
    ).astype(jnp.bfloat16)
    query, kv = project(
        normed, w_query, w_key, w_value, cosine, sine, sort, exchange, group_count
    )
    if not exchange:
        kv = lax.all_gather(kv[0], "dp", axis=0)
    context = attend(
        bounds, query, kv, key_place, my_sorted[:, None], my_start[:, None], back, key_rows, q_rows
    )
    return project_out(context, w_output, tokens)


def solution(mesh):
    placed = (
        P(("dp", "tp"), None),
        P(),
        P(None, "tp"),
        P(None, "tp"),
        P(None, "tp"),
        P("tp", None),
        P(),
        P(),
    )
    return jax.shard_map(
        body, mesh=mesh, in_specs=placed, out_specs=P(("dp", "tp"), None), check_vma=False
    )
```

time: 411 us -> 230 us (0.56)
  waiting for transfers between devices: 265 us -> 0 us
  Pallas kernels: 0 us -> 209 us
  matrix products: 66.4 us -> 0 us
  local copies, waits for them, and re-layouts: 32.1 us -> 8.05 us
  between operations: 13.6 us -> 0.06 us
  starting transfers between devices: 11.9 us -> 0 us
  other arithmetic: 21 us -> 12.5 us
    pallas_call x0 -> x3, Pallas kernels: none -> 209 us  [the longest x1 107 us: project(): pl.pallas_call(functools.partial(project_kernel, exchange), out_shape=(ja...]
    all_to_all x2 -> x0, waiting for transfers between devices: 186 us -> none  [the longest x1 160 us: body(): lax.all_to_all(fanned.reshape(slot_total, model_width), ('dp', 'tp'), spl...]
    reduce_scatter x1 -> x0, waiting for transfers between devices: 78.4 us -> none  [body(): lax.psum_scatter(jnp.dot(compact, w_output, preferred_element_type=jnp.fl...]
    dot_general x6 -> x0, matrix products: 44.3 us -> none  [the longest x1 13 us: body(): jnp.dot(arrived, w_query, preferred_element_type=jnp.float32)]
    sub x2 -> x0, matrix products: 22.1 us -> none  [attend(): weights = jnp.exp(score_values - row_peak)]
    dot_general x2 -> x0, local copies, waits for them, and re-layouts: 15.4 us -> none  [the longest x1 11.3 us: body(): jnp.dot(arrived, w_query, preferred_element_type=jnp.float32)]
    all_to_all x2 -> x0, starting transfers between devices: 11.9 us -> none  [the longest x1 7.63 us: body(): lax.all_to_all(fanned.reshape(slot_total, model_width), ('dp', 'tp'), spl...]
    another operation x5 -> x3, other arithmetic: 5.25 us -> 0.78 us  [the longest x1 0.61 us: body(): jnp.stack([jnp.sum((chunk_high[None, :] < tile_low[:, None]).astype(jnp.i...]
  transfers between devices with their start and end apart: 3 -> 0, of which waited for: 3 -> 0; matrix products, arithmetic and copies ran while one was open for 5% -> 0% of each run, Pallas kernels for 0% -> 0%
where the time goes in v1:
time: 230 us; the launch traced here: 229 us
  Pallas kernels  209 us (91%)
  other arithmetic  12.5 us (5%)
  local copies, waits for them, and re-layouts  8.05 us (4%)
    pallas_call x1, Pallas kernels, project(): pl.pallas_call(functools.partial(project_kernel, exchange), out_shape=(ja...  107 us
    pallas_call x1, Pallas kernels, project_out(): pl.pallas_call(output_kernel, out_shape=jax.ShapeDtypeStruct(tokens.shape...  82.5 us
    pallas_call x1, Pallas kernels, attend(): pl.pallas_call(functools.partial(attend_kernel, key_rows, q_rows), out_sh...  18.8 us

profile of v1, /device:TPU:0, one launch (start us, length us, event | category | flops | bytes accessed | tf_op | source)
XLA Modules:
  0.0 229.2 jit_solution(2152706427149997411)
XLA Ops:
  0.0 0.7 lt.28
  0.7 1.3 convert_reduce_fusion
  2.1 1.1 select_reduce_fusion
  3.4 0.5 broadcast.33
  3.9 0.7 fusion.7
  4.6 0.2 slice_reduce_fusion
  4.8 0.2 convert_reduce_fusion.1
  5.2 0.7 copy.18
  6.1 0.7 sub.10
  7.1 0.2 convert_reduce_fusion.2
  7.3 0.6 pad_add_fusion.bounds_ref
  7.9 1.5 fusion
  9.4 2.5 %fusion.2.x_ref = bf16[128,4096]{1,0:T(8,128)(2,1)} fusion(bf16[128,4096]{1,0:T(8,128)(2,1)} %tokens_ref.1, f32[4096]{0:T(1024)} %param.9, f32[128]{0:T(128)S(1)} %add_rsqrt_fusion), kind=kLoop, calls=%fused_computation.7 | loop fusion | flops 2097152 | bytes 2114048 | tf_op jit(solution)/shard_map/convert_element_type | solution.py:433
  11.9 1.0 fusion.5
  12.9 0.8 pad_maximum_fusion.cos_ref
  13.8 0.8 pad_maximum_fusion.1.sin_ref
  14.6 1.2 fusion.4
  15.8 107.3 %project.1 = (bf16[512,1024]{1,0:T(8,128)(2,1)}, bf16[8,512,512]{2,1,0:T(8,128)(2,1)}) custom-call(bf16[128,4096]{1,0:T(8,128)(2,1)} %fusion.2.x_ref, bf16[4096,1024]{1,0:T(8,128)(2,1)} %wq_ref.1, bf16[4096,256]{1,0:T(8,128)(2,1)} %wk_ref.1, bf16[4096,256]{1,0:T(8,128)(2,1)} %wv_ref.1, f32[512,128]{1,0:T(8,128)} %pad_maximum_fusion.cos_ref, ...), custom_call_target="tpu_custom_call" | custom-call | tf_op jit(solution)/shard_map/project/pallas_call | solution.py:161
  123.2 0.7 reshape.78.key_place_ref
  123.9 0.9 copy.20.q_place_ref
  124.8 0.9 copy.21.q_start_ref
  125.6 18.8 %attend.1.context_ref = bf16[512,1024]{1,0:T(8,128)(2,1)} custom-call(s32[2,8]{1,0:T(2,128)} %pad_add_fusion.bounds_ref, bf16[512,1024]{1,0:T(8,128)(2,1)} %get-tuple-element.7.q_ref, bf16[8,512,512]{2,1,0:T(8,128)(2,1)} %get-tuple-element.8.kv_ref, s32[8,1,512]{2,1,0:T(1,128)} %reshape.78.key_place_ref, s32[512,1]{1,0:T(8,128)} %copy.20.q_place_ref, ...), custom_call_target="tpu_custom_call" | custom-call | tf_op jit(solution)/shard_map/attend/pallas_call | solution.py:273
  144.4 82.5 %project_out.1 = bf16[128,4096]{1,0:T(8,128)(2,1)} custom-call(bf16[512,1024]{1,0:T(8,128)(2,1)} %attend.1.context_ref, bf16[1024,4096]{1,0:T(8,128)(2,1)} %w_ref.1, bf16[128,4096]{1,0:T(8,128)(2,1)} %tokens_ref.1), custom_call_target="tpu_custom_call" | custom-call | tf_op jit(solution)/shard_map/project_out/pallas_call | solution.py:359
  226.9 2.3 copy.23
  (17 shorter events, 1.1 us)

commit v2 on v1

--- a/solution.py
+++ b/solution.py
@@ -38,23 +38,30 @@
 
 
 def project_kernel(
-    exchange, x_ref, wq_ref, wk_ref, wv_ref, cos_ref, sin_ref, sort_ref,
-    q_out, kv_out, gathered, mixed_q, mixed_kv, send_sem, recv_sem, kv_send, kv_recv,
+    exchange, x_ref, wq_hbm, wk_hbm, wv_hbm, cos_ref, sin_ref,
+    q_out, kv_out, gathered, wq_ref, wk_ref, wv_ref,
+    own_sem, send_sem, recv_sem, load_sem, kv_send, kv_recv,
 ):
     tok = x_ref.shape[0]
-    half = tok // 2
     dp = lax.axis_index("dp")
     me = lax.axis_index("tp")
+    last = 3
     right, left = lax.rem(me + 1, 4), lax.rem(me + 3, 4)
-    far = lax.rem(me + 2, 4)
-    go_right, go_left = (dp, right), (dp, left)
     core = lax.rem(dp, 2)
     x_at = lax.rem(dp // 2, 2)
     y_at = dp // 4
     mate = dp + 1 - 2 * core
     x_near = dp + 2 - 4 * x_at
     y_near = dp + 4 - 8 * y_at
-    peers = [go_right, go_left]
+    cross = x_near + y_near - dp
+    loads = [
+        pltpu.make_async_copy(wk_hbm, wk_ref, load_sem.at[0]),
+        pltpu.make_async_copy(wv_hbm, wv_ref, load_sem.at[1]),
+        pltpu.make_async_copy(wq_hbm, wq_ref, load_sem.at[2]),
+    ]
+    for load in loads:
+        load.start()
+    peers = [(dp, right), (dp, left)]
     if exchange:
         peers += [(mate, me), (x_near, me), (y_near, me)]
     greet(peers)
@@ -62,124 +69,183 @@
     def rows(owner, start=0, size=tok):
         return pl.ds(pl.multiple_of(owner * tok + start, size), size)
 
-    own_right = remote(x_ref, gathered.at[rows(me)], send_sem.at[0], recv_sem.at[0], go_right)
-    own_left = remote(x_ref, gathered.at[rows(me)], send_sem.at[1], recv_sem.at[1], go_left)
-    own_right.start()
-    own_left.start()
-
-    def project(owner, block):
+    own_right = remote(x_ref, gathered.at[rows(me)], own_sem.at[0], recv_sem.at[me], (dp, right))
+    own_left = remote(x_ref, gathered.at[rows(me)], own_sem.at[1], recv_sem.at[me], (dp, left))
+
+    @pl.when(me < last)
+    def _():
+        own_right.start()
+
+    @pl.when(me > 0)
+    def _():
+        own_left.start()
+
+    order = ((0, 1, 2, 3), (1, 0, 2, 3), (2, 1, 3, 0), (3, 2, 1, 0))
+
+    def owner_at(k):
+        code = sum(order[m][k] << (2 * m) for m in range(4))
+        return lax.rem(lax.shift_right_logical(jnp.int32(code), 2 * me), 4)
+
+    def passing(owner, where):
+        block = gathered.at[rows(owner)]
+        return remote(block, block, send_sem.at[owner], recv_sem.at[owner], (dp, where))
+
+    def receive(k):
+        owner = owner_at(k)
+        passing(owner, right).wait_recv()
+
+        @pl.when((owner < me) & (me < last))
+        def _():
+            passing(owner, right).start()
+
+        @pl.when((owner > me) & (me > 0))
+        def _():
+            passing(owner, left).start()
+
+    own_slot = dp if exchange else 0
+    kv_width = wk_ref.shape[1]
+
+    def turn(owner, tile):
         cosine = cos_ref[rows(owner), :]
         sine = sin_ref[rows(owner), :]
-
-        def turn(tile):
-            heads = []
-            for h in range(tile.shape[1] // HEAD_DIM):
-                head = tile[:, h * HEAD_DIM : (h + 1) * HEAD_DIM]
-                heads.append(head * cosine + pltpu.roll(head, HEAD_DIM // 2, 1) * sine)
-            return jnp.concatenate(heads, axis=1).astype(jnp.bfloat16)
-
-        kv_width = wk_ref.shape[1]
+        heads = []
+        for h in range(tile.shape[1] // HEAD_DIM):
+            head = tile[:, h * HEAD_DIM : (h + 1) * HEAD_DIM]
+            heads.append(head * cosine + pltpu.roll(head, HEAD_DIM // 2, 1) * sine)
+        return jnp.concatenate(heads, axis=1).astype(jnp.bfloat16)
+
+    def project_kv(owner, block):
         keys = jnp.dot(block[...], wk_ref[...], preferred_element_type=jnp.float32)
-        mixed_kv[rows(owner), pl.ds(0, kv_width)] = turn(keys)
+        kv_out[own_slot, rows(owner), pl.ds(0, kv_width)] = turn(owner, keys)
         values = jnp.dot(block[...], wv_ref[...], preferred_element_type=jnp.float32)
-        mixed_kv[rows(owner), pl.ds(kv_width, kv_width)] = values.astype(jnp.bfloat16)
-
+        kv_out[own_slot, rows(owner), pl.ds(kv_width, kv_width)] = values.astype(jnp.bfloat16)
+
+    def project_q(owner, block):
         def step(i, _):
             columns = pl.ds(pl.multiple_of(i * 256, 256), 256)
             tile = jnp.dot(block[...], wq_ref[:, columns], preferred_element_type=jnp.float32)
-            mixed_q[rows(owner), columns] = turn(tile)
+            q_out[rows(owner), columns] = turn(owner, tile)
             return 0
 
         lax.fori_loop(0, wq_ref.shape[1] // 256, step, 0)
 
-    project(me, x_ref)
-    own_right.wait_recv()
-    top = gathered.at[rows(left, 0, half)]
-    pass_right = remote(top, top, send_sem.at[2], recv_sem.at[2], go_right)
-    pass_right.start()
-    own_left.wait_recv()
-    low = gathered.at[rows(right, half, half)]
-    pass_left = remote(low, low, send_sem.at[3], recv_sem.at[3], go_left)
-    pass_left.start()
-    project(left, gathered.at[rows(left)])
-    project(right, gathered.at[rows(right)])
-    pass_right.wait_recv()
-    pass_left.wait_recv()
-    project(far, gathered.at[rows(far)])
-
-    own = kv_out.at[dp] if exchange else kv_out.at[0]
-    own[...] = jnp.dot(
-        sort_ref[...], mixed_kv[...], preferred_element_type=jnp.float32
-    ).astype(jnp.bfloat16)
-    started = [own_right, own_left, pass_right, pass_left]
+    half = tok // 2
+    started = []
+
+    def put(ref, k, i, where):
+        copy = remote(ref, ref, kv_send.at[k, i], kv_recv.at[k, i], (where, me))
+        copy.start()
+        started.append(copy)
+        return copy
+
+    def first_sends(k):
+        block = kv_out.at[dp, rows(owner_at(k))]
+        return put(block, k, 0, x_near), put(block, k, 1, y_near), put(block, k, 2, mate)
+
+    def second_sends(k, sent):
+        owner = owner_at(k)
+        to_x, to_y, to_mate = sent
+        to_x.wait_recv()
+        x_over = put(kv_out.at[x_near, rows(owner, 0, half)], k, 3, y_near)
+        x_mate = put(kv_out.at[x_near, rows(owner)], k, 4, mate)
+        to_y.wait_recv()
+        y_over = put(kv_out.at[y_near, rows(owner, half, half)], k, 5, x_near)
+        y_mate = put(kv_out.at[y_near, rows(owner)], k, 6, mate)
+        return owner, (x_over, y_over), (to_mate, x_mate, y_mate)
+
+    def third_sends(k, sent):
+        owner, (x_over, y_over), others = sent
+        x_over.wait_recv()
+        up_mate = put(kv_out.at[cross, rows(owner, 0, half)], k, 7, mate)
+        y_over.wait_recv()
+        low_mate = put(kv_out.at[cross, rows(owner, half, half)], k, 8, mate)
+        return others + (up_mate, low_mate)
+
+    ends = []
+    for load in loads:
+        load.wait()
+    project_kv(me, x_ref)
     if exchange:
-        span = kv_out.shape[1]
-        upper, lower = pl.ds(0, span // 2), pl.ds(span // 2, span // 2)
-        cross = x_near + y_near - dp
-
-        def put(ref, i, where):
-            copy = remote(ref, ref, kv_send.at[i], kv_recv.at[i], (where, me))
-            copy.start()
-            return copy
-
-        to_x = put(kv_out.at[dp], 0, x_near)
-        to_y = put(kv_out.at[dp], 1, y_near)
-        to_mate = put(kv_out.at[dp], 2, mate)
-
-    def sort_step(i, _):
-        columns = pl.ds(pl.multiple_of(i * 256, 256), 256)
-        q_out[:, columns] = jnp.dot(
-            sort_ref[...], mixed_q[:, columns], preferred_element_type=jnp.float32
-        ).astype(jnp.bfloat16)
-        return 0
-
-    lax.fori_loop(0, wq_ref.shape[1] // 256, sort_step, 0)
-
+        sent0 = first_sends(0)
+    project_q(me, x_ref)
     if exchange:
-        to_x.wait_recv()
-        x_over = put(kv_out.at[x_near, upper], 3, y_near)
-        x_mate = put(kv_out.at[x_near], 4, mate)
-        to_y.wait_recv()
-        y_over = put(kv_out.at[y_near, lower], 5, x_near)
-        y_mate = put(kv_out.at[y_near], 6, mate)
-        x_over.wait_recv()
-        up_mate = put(kv_out.at[cross, upper], 7, mate)
-        y_over.wait_recv()
-        low_mate = put(kv_out.at[cross, lower], 8, mate)
-        for copy in (to_mate, x_mate, y_mate, up_mate, low_mate):
-            copy.wait_recv()
-        started += [to_x, to_y, to_mate, x_over, x_mate, y_over, y_mate, up_mate, low_mate]
+        sent0 = second_sends(0, sent0)
+    receive(1)
+    receive(2)
+    if exchange:
+        ends += third_sends(0, sent0)
+    waiting = []
+    for k in (1, 2, 3):
+        owner = owner_at(k)
+        if k == 3:
+            receive(3)
+        project_kv(owner, gathered.at[rows(owner)])
+        if exchange:
+            sent = first_sends(k)
+            for j, old in waiting:
+                ends += third_sends(j, old)
+            waiting = []
+        if k == 3 and exchange:
+            sent = second_sends(k, sent)
+        project_q(owner, gathered.at[rows(owner)])
+        if exchange:
+            if k < 3:
+                sent = second_sends(k, sent)
+            waiting = [(k, sent)]
+    for j, old in waiting:
+        ends += third_sends(j, old)
+    for copy in ends:
+        copy.wait_recv()
     for copy in started:
         copy.wait_send()
 
-
-def project(normed, w_query, w_key, w_value, cosine, sine, sort, exchange, group_count):
+    @pl.when(me < last)
+    def _():
+        own_right.wait_send()
+
+    @pl.when(me > 0)
+    def _():
+        own_left.wait_send()
+
+    for k in (1, 2, 3):
+        owner = owner_at(k)
+
+        @pl.when(((owner < me) & (me < last)) | ((owner > me) & (me > 0)))
+        def _():
+            passing(owner, right).wait_send()
+
+
+def project(normed, w_query, w_key, w_value, cosine, sine, exchange, group_count):
     tok, width = normed.shape
     span = 4 * tok
     q_width, kv_width = w_query.shape[1], w_key.shape[1]
     slots = group_count if exchange else 1
+    hbm = pl.BlockSpec(memory_space=pl.ANY)
     return pl.pallas_call(
         functools.partial(project_kernel, exchange),
         out_shape=(
             jax.ShapeDtypeStruct((span, q_width), jnp.bfloat16),
             jax.ShapeDtypeStruct((slots, span, 2 * kv_width), jnp.bfloat16),
         ),
-        in_specs=[VMEM_SPEC] * 7,
+        in_specs=[VMEM_SPEC, hbm, hbm, hbm, VMEM_SPEC, VMEM_SPEC],
         out_specs=(VMEM_SPEC, VMEM_SPEC),
         scratch_shapes=[
             pltpu.VMEM((span, width), jnp.bfloat16),
-            pltpu.VMEM((span, q_width), jnp.bfloat16),
-            pltpu.VMEM((span, 2 * kv_width), jnp.bfloat16),
+            pltpu.VMEM(w_query.shape, jnp.bfloat16),
+            pltpu.VMEM(w_key.shape, jnp.bfloat16),
+            pltpu.VMEM(w_value.shape, jnp.bfloat16),
+            pltpu.SemaphoreType.DMA((2,)),
             pltpu.SemaphoreType.DMA((4,)),
             pltpu.SemaphoreType.DMA((4,)),
-            pltpu.SemaphoreType.DMA((9,)),
-            pltpu.SemaphoreType.DMA((9,)),
+            pltpu.SemaphoreType.DMA((3,)),
+            pltpu.SemaphoreType.DMA((4, 9)),
+            pltpu.SemaphoreType.DMA((4, 9)),
         ],
         compiler_params=pltpu.CompilerParams(
             collective_id=0, has_side_effects=True, vmem_limit_bytes=VMEM_BYTES
         ),
         name="project",
-    )(normed, w_query, w_key, w_value, cosine, sine, sort)
+    )(normed, w_query, w_key, w_value, cosine, sine)
 
 
 def attend_kernel(
@@ -188,7 +254,9 @@
 ):
     sources = kv_ref.shape[0]
     kv_count = kv_ref.shape[2] // (2 * HEAD_DIM)
-    group = q_ref.shape[1] // HEAD_DIM // kv_count
+    blocks, block_rows, width = q_ref.shape
+    group = width // HEAD_DIM // kv_count
+    piece = q_rows // blocks
     chunk = sources * key_rows
     scale = HEAD_DIM ** (-0.5) * LOG2E
     stack = group * q_rows
@@ -197,12 +265,15 @@
         at = pl.ds(pl.multiple_of(t * q_rows, q_rows), q_rows)
         place = q_place_ref[at, :]
         start = q_start_ref[at, :]
+        inner = pl.ds(pl.multiple_of(t * piece, piece), piece)
         queries = []
         for h in range(kv_count):
             queries.append(
                 jnp.concatenate(
                     [
-                        q_ref[at, (h * group + j) * HEAD_DIM : (h * group + j + 1) * HEAD_DIM]
+                        q_ref[
+                            :, inner, (h * group + j) * HEAD_DIM : (h * group + j + 1) * HEAD_DIM
+                        ].reshape(q_rows, HEAD_DIM)
                         for j in range(group)
                     ],
                     axis=0,
@@ -254,19 +325,17 @@
             done = (mixed / total).astype(jnp.bfloat16)
             for j in range(group):
                 head = (h * group + j) * HEAD_DIM
-                context[at, head : head + HEAD_DIM] = done[j * q_rows : (j + 1) * q_rows]
+                context[:, inner, head : head + HEAD_DIM] = done[
+                    j * q_rows : (j + 1) * q_rows
+                ].reshape(blocks, piece, HEAD_DIM)
         return 0
 
-    lax.fori_loop(0, q_ref.shape[0] // q_rows, tile_step, 0)
-
-    def back_step(i, _):
-        columns = pl.ds(pl.multiple_of(i * 256, 256), 256)
-        out_ref[:, columns] = jnp.dot(
-            back_ref[...], context[:, columns], preferred_element_type=jnp.float32
+    lax.fori_loop(0, block_rows // piece, tile_step, 0)
+
+    for j in range(blocks):
+        out_ref[j] = jnp.dot(
+            back_ref[j], context[j], preferred_element_type=jnp.float32
         ).astype(jnp.bfloat16)
-        return 0
-
-    lax.fori_loop(0, q_ref.shape[1] // 256, back_step, 0)
 
 
 def attend(bounds, query, kv_all, key_place, q_place, q_start, back, key_rows, q_rows):
@@ -378,19 +447,20 @@
     my_group = lax.axis_index("dp")
     exchange = group_count == 8
     q_rows = 64
-    key_rows = max(16, 512 // group_count)
-    key_chunks = span // key_rows
-
-    packs = pack_index.reshape(group_count, span)
-    order = jnp.arange(span, dtype=jnp.int32)
+    source_count = group_count * tp_count
+    key_rows = max(16, 512 // source_count)
+    key_chunks = tok_dev // key_rows
+
+    packs = pack_index.reshape(source_count, tok_dev)
+    order = jnp.arange(tok_dev, dtype=jnp.int32)
     rank = jnp.sum((packs[:, None, :] < packs[:, :, None]).astype(jnp.int32), axis=2)
     sorted_packs = jnp.sum(
         jnp.where(rank[:, None, :] == order[None, :, None], packs[:, None, :], 0), axis=2
     )
     key_place = (
-        sorted_packs.reshape(group_count, key_chunks, key_rows)
+        sorted_packs.reshape(source_count, key_chunks, key_rows)
         .transpose(1, 0, 2)
-        .reshape(key_chunks, 1, group_count * key_rows)
+        .reshape(key_chunks, 1, source_count * key_rows)
     )
     chunk_low = jnp.min(key_place, axis=(1, 2))
     chunk_high = jnp.max(key_place, axis=(1, 2))
@@ -402,14 +472,20 @@
         inside = (place[:, None] >= doc_starts[None, :]) & (place[:, None] < doc_ends[None, :])
         return jnp.sum(jnp.where(inside, doc_starts[None, :], 0), axis=1)
 
-    my_pack = lax.dynamic_index_in_dim(packs, my_group, 0, keepdims=False)
-    my_rank = lax.dynamic_index_in_dim(rank, my_group, 0, keepdims=False)
-    my_sorted = lax.dynamic_index_in_dim(sorted_packs, my_group, 0, keepdims=False)
-    sort = (my_rank[None, :] == order[:, None]).astype(jnp.bfloat16)
-    back = (my_rank[:, None] == order[None, :]).astype(jnp.bfloat16)
-    my_start = start_of(my_sorted)
-    tile_low = my_start.reshape(-1, q_rows)[:, 0]
-    tile_high = my_sorted.reshape(-1, q_rows)[:, -1]
+    my_rank = lax.dynamic_slice_in_dim(rank, my_group * tp_count, tp_count)
+    my_sorted = lax.dynamic_slice_in_dim(sorted_packs, my_group * tp_count, tp_count)
+    own_rank = lax.dynamic_index_in_dim(my_rank, lax.axis_index("tp"), 0, keepdims=False)
+    sort = (own_rank[None, :] == order[:, None]).astype(jnp.bfloat16)
+    back = (my_rank[:, :, None] == order[None, None, :]).astype(jnp.bfloat16)
+    my_pack = my_sorted.reshape(span)
+    my_start = start_of(my_pack)
+
+    def by_tile(rows):
+        pieces = rows.reshape(tp_count, -1, q_rows // tp_count)
+        return pieces.transpose(1, 0, 2).reshape(-1, q_rows)
+
+    q_place, q_start = by_tile(my_pack), by_tile(my_start)
+    tile_low, tile_high = jnp.min(q_start, axis=1), jnp.max(q_place, axis=1)
     bounds = jnp.stack(
         [
             jnp.sum((chunk_high[None, :] < tile_low[:, None]).astype(jnp.int32), axis=1),
@@ -417,7 +493,7 @@
         ]
     )
 
-    position = my_pack - start_of(my_pack)
+    position = my_pack - my_start
     half_dim = HEAD_DIM // 2
     frequency = rope_base ** (-2.0 * jnp.arange(half_dim, dtype=jnp.float32) / HEAD_DIM)
     angles = position.astype(jnp.float32)[:, None] * frequency[None, :]
@@ -431,15 +507,22 @@
         * lax.rsqrt(jnp.mean(residual * residual, axis=1, keepdims=True) + norm_eps)
         * norm_gain
     ).astype(jnp.bfloat16)
-    query, kv = project(
-        normed, w_query, w_key, w_value, cosine, sine, sort, exchange, group_count
-    )
+    normed = jnp.dot(sort, normed, preferred_element_type=jnp.float32).astype(jnp.bfloat16)
+    query, kv = project(normed, w_query, w_key, w_value, cosine, sine, exchange, group_count)
     if not exchange:
         kv = lax.all_gather(kv[0], "dp", axis=0)
     context = attend(
-        bounds, query, kv, key_place, my_sorted[:, None], my_start[:, None], back, key_rows, q_rows
-    )
-    return project_out(context, w_output, tokens)
+        bounds,
+        query.reshape(tp_count, tok_dev, -1),
+        kv.reshape(source_count, tok_dev, -1),
+        key_place,
+        q_place.reshape(span, 1),
+        q_start.reshape(span, 1),
+        back,
+        key_rows,
+        q_rows,
+    )
+    return project_out(context.reshape(span, -1), w_output, tokens)
 
 
 def solution(mesh):

time: 230 us -> 208 us (0.904)
  Pallas kernels: 209 us -> 191 us
  other arithmetic: 12.5 us -> 9.58 us
    pallas_call x1, Pallas kernels: 107 us -> 89.7 us  [project(): pl.pallas_call(functools.partial(project_kernel, exchange), out_shape=(ja...]
    convert_element_type x2 -> x1, other arithmetic: 3.7 us -> 0.79 us  [body(): back = (my_rank[:, :, None] == order[None, None, :]).astype(jnp.bfloat16)]
where the time goes in v2:
time: 208 us
  Pallas kernels  191 us (92%)
  other arithmetic  9.58 us (5%)
  local copies, waits for them, and re-layouts  6.12 us (3%)
    pallas_call x1, Pallas kernels, project(): pl.pallas_call(functools.partial(project_kernel, exchange), out_shape=(ja...  89.7 us
    pallas_call x1, Pallas kernels, project_out(): pl.pallas_call(output_kernel, out_shape=jax.ShapeDtypeStruct(tokens.shape...  83.4 us
    pallas_call x1, Pallas kernels, attend(): pl.pallas_call(functools.partial(attend_kernel, key_rows, q_rows), out_sh...  17.8 us

profile of v2, /device:TPU:0, one launch (start us, length us, event | category | flops | bytes accessed | tf_op | source)
XLA Modules:
  0.0 208.2 jit_solution(2951556428380103013)
XLA Ops:
  0.0 2.1 %convert_reduce_fusion = s32[32,128]{1,0:T(8,128)S(1)} fusion(s32[32,128]{1,0:T(8,128)} %bitcast.20), kind=kLoop, calls=%fused_computation.8 | loop fusion | flops 1568768 | bytes 32768 | tf_op jit(solution)/shard_map/reduce_sum | solution.py:456
  2.1 1.3 select_reduce_fusion
  3.5 0.7 copy.27
  4.4 0.7 sub.10
  5.2 1.0 fusion.7
  6.2 0.9 pad_maximum_fusion.1.sin_ref
  7.0 0.8 pad_maximum_fusion.cos_ref
  7.9 0.3 fusion
  8.2 1.5 convolution_convert_fusion.x_ref
  9.7 89.7 %project.1 = (bf16[512,1024]{1,0:T(8,128)(2,1)}, bf16[8,512,512]{2,1,0:T(8,128)(2,1)}) custom-call(bf16[128,4096]{1,0:T(8,128)(2,1)} %convolution_convert_fusion.x_ref, bf16[4096,1024]{1,0:T(8,128)(2,1)} %wq_hbm.1, bf16[4096,256]{1,0:T(8,128)(2,1)} %wk_hbm.1, bf16[4096,256]{1,0:T(8,128)(2,1)} %wv_hbm.1, f32[512,128]{1,0:T(8,128)} %pad_maximum_fusion.cos_ref, ...), custom_call_target="tpu_custom_call" | custom-call | tf_op jit(solution)/shard_map/project/pallas_call | solution.py:224
  99.4 0.1 reduce_min.21
  99.6 0.1 reduce_max.25
  99.8 0.2 convert_reduce_fusion.2
  100.0 0.1 reduce_max.37
  100.2 0.1 reduce_min.28
  100.4 0.2 convert_reduce_fusion.1
  100.5 0.5 pad_add_fusion.bounds_ref
  101.1 0.9 reshape_reshape.13.q_start_ref
  102.1 0.9 reshape_reshape.12.q_place_ref
  102.9 0.8 fusion.6.back_ref
  103.9 0.7 reshape.87.key_place_ref
  104.6 17.8 %attend.1 = bf16[4,128,1024]{2,1,0:T(8,128)(2,1)} custom-call(s32[2,8]{1,0:T(2,128)} %pad_add_fusion.bounds_ref, bf16[4,128,1024]{2,1,0:T(8,128)(2,1)} %bitcast.18, bf16[32,128,512]{2,1,0:T(8,128)(2,1)} %bitcast.16, s32[8,1,512]{2,1,0:T(1,128)} %reshape.87.key_place_ref, s32[512,1]{1,0:T(8,128)} %reshape_reshape.12.q_place_ref, ...), custom_call_target="tpu_custom_call" | custom-call | tf_op jit(solution)/shard_map/attend/pallas_call | solution.py:342
  122.5 83.4 %project_out.1 = bf16[128,4096]{1,0:T(8,128)(2,1)} custom-call(bf16[512,1024]{1,0:T(8,128)(2,1)} %bitcast.17, bf16[1024,4096]{1,0:T(8,128)(2,1)} %w_ref.1, bf16[128,4096]{1,0:T(8,128)(2,1)} %tokens_ref.1), custom_call_target="tpu_custom_call" | custom-call | tf_op jit(solution)/shard_map/project_out/pallas_call | solution.py:428
  205.9 2.3 %copy.36 = bf16[128,4096]{1,0:T(8,128)(2,1)} copy(bf16[128,4096]{1,0:T(8,128)(2,1)} %project_out.1) | data formatting | bytes 2097152
  (22 shorter events, 0.9 us)
Async XLA Ops:
  0.0 7.9 %copy-start = (bf16[128,4096]{1,0:T(8,128)(2,1)S(1)}, bf16[128,4096]{1,0:T(8,128)(2,1)}, u32[]{:S(2)}) copy-start(bf16[128,4096]{1,0:T(8,128)(2,1)} %tokens_ref.1) | copy-start | bytes 3145732
  0.0 8.2 %copy-start.1 = (f32[4096]{0:T(1024)S(1)}, f32[4096]{0:T(1024)}, u32[]{:S(2)}) copy-start(f32[4096]{0:T(1024)} %param.9) | copy-start | bytes 49156
